TPU v7x, 32 devices: a whole 2x2x4 slice. The times are simulated.
32 devices in a mesh: tm: 16 (over z, y, x), rows: 2 (over core).
Axes of the slice: x: 2, y: 2, z: 4, core: 2. Of those that a mesh axis runs over, the one named last changes fastest.
Arguments:
- resid: float32 [2, 16, 16, 512], P(None, 'tm', 'rows'), may hold values from -3 to 3
- basis: float32 [4, 2, 16, 16, 512], P(None, None, 'tm', 'rows'), may hold values from -0.01171875 to 0.01171875
Outputs:
- precond: float32 [2, 16, 16, 512], P(None, 'tm', 'rows')
- image: float32 [2, 16, 16, 512], P(None, 'tm', 'rows')
- gram: float32 [5], replicated
All inputs are finite; a program needn't handle non-finite values.
Results may differ from a plain program's by a relative error of at most 0.0005.
Values sent between devices are 32-bit elements; how exact they have to be, the bound alone decides.
A program may use at most 64 MiB of HBM per device.

v0:
```python
import math

import jax
import jax.numpy as jnp
from jax import lax
from jax.sharding import PartitionSpec as P

SWEEPS = 4


ALPHA = 0.01


def padded_2(shard, sides, width):
    for axis, dim in sides:
        count, length = (lax.axis_size(axis), shard.shape[dim])
        up = [(i, (i + 1) % count) for i in range(count - 1)]
        down = [(j, i) for i, j in up]
        last = lax.slice_in_dim(shard, length - width, length, axis=dim)
        first = lax.slice_in_dim(shard, 0, width, axis=dim)
        before = lax.ppermute(last, axis, up)
        after = lax.ppermute(first, axis, down)
        shard = jnp.concatenate([before, shard, after], axis=dim)
    return shard


def shifted(value, axis, steps):
    count = lax.axis_size(axis)
    first, last = (max(0, -steps), min(count, count - steps))
    return lax.ppermute(value, axis, [(source, source + steps) for source in range(first, last)])


def neighbours(padded):
    middle = padded[:, 1:-1]
    sides = jnp.pad(middle, ((0, 0), (0, 0), (1, 1)))
    return padded[:, 2:] + padded[:, :-2] + sides[:, :, 2:] + sides[:, :, :-2]


def cmul(left, right_re, right_im):
    return jnp.stack(
        [left[0] * right_re - left[1] * right_im, left[0] * right_im + left[1] * right_re]
    )


def phases(first, second, steps):
    turns = first * second % steps
    angle = turns.astype(jnp.float32) * (2.0 * math.pi / steps)
    return (jnp.cos(angle), jnp.sin(angle))


def on_device(resid, basis):
    steps = lax.axis_size("tm")
    coupling = 16.0 / (steps * steps)
    me = lax.axis_index("tm")
    rows_dev = resid.shape[2]
    cols = resid.shape[3]
    cells = rows_dev * cols
    piece = cells // steps
    mine = me.astype(jnp.float32)
    gamma = jnp.power(jnp.float32(ALPHA), mine / steps)
    scaled = resid[:, 0] * gamma
    ordinal = jnp.arange(steps, dtype=jnp.int32)
    cos_table, sin_table = phases(ordinal[:, None], ordinal[None, :], steps)
    blocks = lax.all_to_all(
        scaled.reshape(1, 2, cells), "tm", split_axis=2, concat_axis=0, tiled=True
    )
    flat = blocks.reshape(steps, 2 * piece)
    real_part = jnp.dot(cos_table, flat, precision=lax.Precision.HIGHEST)
    imag_part = -jnp.dot(sin_table, flat, precision=lax.Precision.HIGHEST)
    stacked = jnp.stack([real_part, imag_part], 1).reshape(steps, 2, 2, piece)
    spectrum = lax.all_to_all(stacked, "tm", split_axis=0, concat_axis=3, tiled=True)
    rhat = spectrum[0].reshape(2, 2, rows_dev, cols)
    base = jnp.power(jnp.float32(ALPHA), jnp.float32(1.0) / steps)
    angle = mine * (2.0 * math.pi / steps)
    lam_re = 1.0 - base * jnp.cos(angle)
    lam_im = base * jnp.sin(angle)
    disp_spec = rhat[:, 0]
    right = cmul(disp_spec, lam_re, lam_im) + rhat[:, 1]
    den_re = lam_re * lam_re - lam_im * lam_im + 4.0 * coupling
    den_im = 2.0 * lam_re * lam_im
    magnitude = den_re * den_re + den_im * den_im
    inv_re = den_re / magnitude
    inv_im = -den_im / magnitude
    uhat = cmul(right, inv_re, inv_im)
    for sweep in range(SWEEPS - 1):
        padded = padded_2(uhat, (("rows", 1),), 1)
        uhat = cmul(right + coupling * neighbours(padded), inv_re, inv_im)
    vhat = cmul(uhat, lam_re, lam_im) - disp_spec
    yhat = jnp.stack([uhat, vhat], 1)
    spread = lax.all_to_all(
        yhat.reshape(1, 2, 2, cells), "tm", split_axis=3, concat_axis=0, tiled=True
    )
    real_rows = spread[:, 0].reshape(steps, 2 * piece)
    imag_rows = spread[:, 1].reshape(steps, 2 * piece)
    undo = jnp.power(jnp.float32(ALPHA), -ordinal.astype(jnp.float32) / steps) / steps
    history = jnp.dot(cos_table, real_rows, precision=lax.Precision.HIGHEST) - jnp.dot(
        sin_table, imag_rows, precision=lax.Precision.HIGHEST
    )
    history = (history * undo[:, None]).reshape(steps, 2, piece)
    returned = lax.all_to_all(history, "tm", split_axis=0, concat_axis=2, tiled=True)
    precond = returned[0].reshape(2, rows_dev, cols)
    earlier = shifted(precond, "tm", 1)
    disp_rim = padded_2(precond[0:1], (("rows", 1),), 1)
    laplace = neighbours(disp_rim)[0] - 4.0 * precond[0]
    first = precond[0] - earlier[0] - precond[1]
    second = precond[1] - earlier[1] - coupling * laplace
    image = jnp.stack([first, second])
    inner = jnp.sum(basis[:, :, 0] * image[None], axis=(1, 2, 3))
    count = 2.0 * steps * rows_dev * lax.axis_size("rows") * cols
    squares = jnp.sum(image * image) / count
    local_terms = jnp.concatenate([inner, squares[None]])
    gram = lax.psum(local_terms, ("tm", "rows"))
    return (precond[:, None], image[:, None], gram)


def solution(mesh):
    in_specs = (P(None, "tm", "rows", None), P(None, None, "tm", "rows", None))
    out_specs = (P(None, "tm", "rows", None), P(None, "tm", "rows", None), P())
    return jax.shard_map(
        on_device, mesh=mesh, in_specs=in_specs, out_specs=out_specs, check_vma=False
    )
```

profile of v0, /device:TPU:0, one launch (start us, length us, event | category | flops | bytes accessed | tf_op | source)
XLA Modules:
  0.0 169.4 jit_solution(10434036143663607024)
XLA Ops:
  0.7 0.8 broadcast_multiply_fusion
  1.4 0.6 copy.44
  2.1 0.5 broadcast.139
  2.6 19.4 %reduce.4 = f32[4096,2]{1,0:T(8,128)} reduce(f32[4096,1,2]{2,1,0:T(1,128)S(1)} %bitcast.83, f32[]{:T(128)} %broadcast.139), dimensions={1}, to_apply=%bitcast.65.reduce_sub_computation | reduce | bytes 65540
  22.0 3.0 %reshape.138 = f32[16,1,512]{2,1,0:T(1,128)S(1)} reshape(f32[4096,2]{1,0:T(8,128)} %reduce.4) | data formatting | bytes 65536
  25.0 15.5 %all_to_all.63 = f32[16,1,512]{2,1,0:T(1,128)S(1)} all-to-all(f32[16,1,512]{2,1,0:T(1,128)S(1)} %reshape.138), channel_id=1, replica_groups=mesh['tm'=16,'rows'=2] {'tm'}, dimensions={0} | all-to-all | bytes 65536 | tf_op jit(solution)/shard_map/all_to_all | solution.py:64
  40.5 0.7 reduce.5
  41.3 3.4 %reshape.139 = f32[4096,1,2]{2,1,0:T(1,128)S(1)} reshape(f32[16,512]{1,0:T(8,128)S(1)} %reduce.5) | data formatting | bytes 65536
  44.7 0.6 copy.45
  45.3 0.2 convolution_bitcast_fusion
  45.5 0.2 convolution_negate_fusion
  45.8 0.7 copy.48
  46.5 3.5 %all-to-all-start.1 = ((f32[16,2,2,256]{3,2,1,0:T(2,128)}), f32[16,2,2,256]{3,2,1,0:T(2,128)S(1)}, u32[]{:S(2)}, u32[]{:S(2)}) async-start(f32[16,2,2,256]{3,2,1,0:T(2,128)} %copy.48), calls=%async_computation.1 | async-start | bytes 131072 | tf_op jit(solution)/shard_map/all_to_all | solution.py:71
  50.2 7.2 %all-to-all-done.1 = f32[16,2,2,256]{3,2,1,0:T(2,128)S(1)} async-done(((f32[16,2,2,256]{3,2,1,0:T(2,128)}), f32[16,2,2,256]{3,2,1,0:T(2,128)S(1)}, u32[]{:S(2)}, u32[]{:S(2)}) %all-to-all-start.1) | async-done | bytes 65568 | tf_op jit(solution)/shard_map/all_to_all | solution.py:71
  57.6 1.3 collective-permute-start
  58.9 3.0 %collective-permute-start.1 = (f32[2,1,512]{2,1,0:T(1,128)S(1)}, f32[2,1,512]{2,1,0:T(1,128)S(1)}, u32[]{:S(2)}, u32[]{:S(2)}) collective-permute-start(f32[2,1,512]{2,1,0:T(1,128)S(1)} %get-tuple-element.26), channel_id=1, source_target_pairs={{0,1},{2,3},{4,5},{6,7},{8,9},{10,11},{12,13},{14,15},{16,17},{18,... | collective-permute-start | bytes 12296 | tf_op jit(solution)/shard_map/ppermute | solution.py:21
  61.9 0.0 collective-permute-done
  62.0 0.8 collective-permute-done.1
  62.7 0.1 fusion.5
  62.9 1.3 collective-permute-start.2
  64.2 3.0 %collective-permute-start.3 = (f32[2,1,512]{2,1,0:T(1,128)S(1)}, f32[2,1,512]{2,1,0:T(1,128)S(1)}, u32[]{:S(2)}, u32[]{:S(2)}) collective-permute-start(f32[2,1,512]{2,1,0:T(1,128)S(1)} %get-tuple-element.22), channel_id=1, source_target_pairs={{0,1},{2,3},{4,5},{6,7},{8,9},{10,11},{12,13},{14,15},{16,17},{18,... | collective-permute-start | bytes 12296 | tf_op jit(solution)/shard_map/ppermute | solution.py:21
  67.2 0.8 collective-permute-done.3
  68.0 0.1 fusion.9
  68.1 1.3 collective-permute-start.4
  69.4 3.2 %collective-permute-start.5 = (f32[2,1,512]{2,1,0:T(1,128)S(1)}, f32[2,1,512]{2,1,0:T(1,128)S(1)}, u32[]{:S(2)}, u32[]{:S(2)}) collective-permute-start(f32[2,1,512]{2,1,0:T(1,128)S(1)} %get-tuple-element.18), channel_id=1, source_target_pairs={{0,1},{2,3},{4,5},{6,7},{8,9},{10,11},{12,13},{14,15},{16,17},{18,... | collective-permute-start | bytes 12296 | tf_op jit(solution)/shard_map/ppermute | solution.py:21
  72.7 0.6 collective-permute-done.5
  73.3 0.1 fusion.13
  73.5 4.4 %copy.51 = f32[1,2,2,4096]{2,1,0,3:T(2,128)} copy(f32[1,2,2,4096]{3,1,2,0:T(2,128)S(1)} %pad_maximum_fusion.1) | data formatting | bytes 131072 | tf_op jit(solution)/shard_map/stack | solution.py:89
  77.9 8.1 %reshape.140 = f32[16,1,1024]{2,1,0:T(1,128)} reshape(f32[4096,1,2,2]{3,2,1,0:T(2,128)} %bitcast.81) | data formatting | bytes 131072
  86.0 3.5 %all-to-all-start.2 = ((f32[16,1,1024]{2,1,0:T(1,128)}), f32[16,1,1024]{2,1,0:T(1,128)S(1)}, u32[]{:S(2)}, u32[]{:S(2)}) async-start(f32[16,1,1024]{2,1,0:T(1,128)} %reshape.140), calls=%async_computation.2 | async-start | bytes 131072 | tf_op jit(solution)/shard_map/all_to_all | solution.py:90
  89.5 7.5 %all-to-all-done.2 = f32[16,1,1024]{2,1,0:T(1,128)S(1)} async-done(((f32[16,1,1024]{2,1,0:T(1,128)}), f32[16,1,1024]{2,1,0:T(1,128)S(1)}, u32[]{:S(2)}, u32[]{:S(2)}) %all-to-all-start.2) | async-done | bytes 65568 | tf_op jit(solution)/shard_map/all_to_all | solution.py:90
  97.0 0.8 reduce.6
  97.8 7.7 %reshape.141 = f32[4096,1,2,2]{3,2,1,0:T(2,128)} reshape(f32[16,1024]{1,0:T(8,128)S(1)} %reduce.6) | data formatting | bytes 131072
  105.6 3.6 %copy.57 = f32[1,2,2,16,256]{4,3,2,1,0:T(8,128)S(1)} copy(f32[1,2,2,16,256]{2,1,4,3,0:T(2,128)} %bitcast.82) | data formatting | bytes 131072 | tf_op jit(solution)/shard_map/all_to_all | solution.py:90
  109.2 0.2 fusion.42
  109.5 0.2 fusion
  109.7 10.0 %all_to_all.64 = f32[16,2,256]{2,1,0:T(2,128)S(1)} all-to-all(f32[16,2,256]{2,1,0:T(2,128)S(1)} %reshape.134), channel_id=1, replica_groups=mesh['tm'=16,'rows'=2] {'tm'}, dimensions={0} | all-to-all | bytes 65536 | tf_op jit(solution)/shard_map/all_to_all | solution.py:100
  119.7 0.1 slice_reduce_fusion
  119.8 2.6 %collective-permute-start.6 = (f32[2,8,512]{2,1,0:T(8,128)S(1)}, f32[2,8,512]{2,1,0:T(8,128)S(1)}, u32[]{:S(2)}, u32[]{:S(2)}) collective-permute-start(f32[2,8,512]{2,1,0:T(8,128)S(1)} %reshape_squeeze.15), channel_id=1, source_target_pairs={{0,2},{2,4},{4,6},{6,8},{8,10},{10,12},{12,14},{14,16},{16,18},{18... | collective-permute-start | bytes 98312 | tf_op jit(solution)/shard_map/ppermute | solution.py:30
  122.4 1.3 collective-permute-start.7
  123.7 3.0 %collective-permute-start.8 = (f32[1,1,512]{2,1,0:T(1,128)S(1)}, f32[1,1,512]{2,1,0:T(1,128)S(1)}, u32[]{:S(2)}, u32[]{:S(2)}) collective-permute-start(f32[1,1,512]{2,1,0:T(1,128)S(1)} %get-tuple-element.30), channel_id=1, source_target_pairs={{0,1},{2,3},{4,5},{6,7},{8,9},{10,11},{12,13},{14,15},{16,17},{18,... | collective-permute-start | bytes 6152 | tf_op jit(solution)/shard_map/ppermute | solution.py:21
  126.8 0.8 collective-permute-done.8
  127.6 0.1 fusion.26
  127.7 1.2 pad_maximum_fusion.18
  129.6 0.1 fusion.1
  129.7 0.1 pad_maximum_fusion.21
  129.8 0.6 broadcast_in_dim_reshape_squeeze.3
  130.4 39.0 %psum.7 = f32[5]{0:T(128)} all-reduce(f32[5]{0:T(128)S(1)} %pad_maximum_fusion.21), channel_id=1, replica_groups=mesh['tm'=16,'rows'=2] {'tm','rows'}, use_global_device_ids=true, to_apply=%region_2.3 | all-reduce | flops 5 | bytes 40 | tf_op jit(solution)/shard_map/psum | solution.py:112
  (42 shorter events, 0.5 us)
Async XLA Ops:
  46.5 11.0 %all-to-all-start.1 = ((f32[16,2,2,256]{3,2,1,0:T(2,128)}), f32[16,2,2,256]{3,2,1,0:T(2,128)S(1)}, u32[]{:S(2)}, u32[]{:S(2)}) async-start(f32[16,2,2,256]{3,2,1,0:T(2,128)} %copy.48), calls=%async_computation.1 | async-start | bytes 131072 | tf_op jit(solution)/shard_map/all_to_all | solution.py:71
  57.6 4.3 %collective-permute-start = (f32[2,1,512]{2,1,0:T(1,128)S(1)}, f32[2,1,512]{2,1,0:T(1,128)S(1)}, u32[]{:S(2)}, u32[]{:S(2)}) collective-permute-start(f32[2,1,512]{2,1,0:T(1,128)S(1)} %get-tuple-element.25), channel_id=1, source_target_pairs={{1,0},{3,2},{5,4},{7,6},{9,8},{11,10},{13,12},{15,14},{17,16},{19,... | collective-permute-start | bytes 12296 | tf_op jit(solution)/shard_map/ppermute | solution.py:22
  58.9 3.8 %collective-permute-start.1 = (f32[2,1,512]{2,1,0:T(1,128)S(1)}, f32[2,1,512]{2,1,0:T(1,128)S(1)}, u32[]{:S(2)}, u32[]{:S(2)}) collective-permute-start(f32[2,1,512]{2,1,0:T(1,128)S(1)} %get-tuple-element.26), channel_id=1, source_target_pairs={{0,1},{2,3},{4,5},{6,7},{8,9},{10,11},{12,13},{14,15},{16,17},{18,... | collective-permute-start | bytes 12296 | tf_op jit(solution)/shard_map/ppermute | solution.py:21
  62.9 4.3 %collective-permute-start.2 = (f32[2,1,512]{2,1,0:T(1,128)S(1)}, f32[2,1,512]{2,1,0:T(1,128)S(1)}, u32[]{:S(2)}, u32[]{:S(2)}) collective-permute-start(f32[2,1,512]{2,1,0:T(1,128)S(1)} %get-tuple-element.21), channel_id=1, source_target_pairs={{1,0},{3,2},{5,4},{7,6},{9,8},{11,10},{13,12},{15,14},{17,16},{19,... | collective-permute-start | bytes 12296 | tf_op jit(solution)/shard_map/ppermute | solution.py:22
  64.2 3.8 %collective-permute-start.3 = (f32[2,1,512]{2,1,0:T(1,128)S(1)}, f32[2,1,512]{2,1,0:T(1,128)S(1)}, u32[]{:S(2)}, u32[]{:S(2)}) collective-permute-start(f32[2,1,512]{2,1,0:T(1,128)S(1)} %get-tuple-element.22), channel_id=1, source_target_pairs={{0,1},{2,3},{4,5},{6,7},{8,9},{10,11},{12,13},{14,15},{16,17},{18,... | collective-permute-start | bytes 12296 | tf_op jit(solution)/shard_map/ppermute | solution.py:21
  68.1 4.5 %collective-permute-start.4 = (f32[2,1,512]{2,1,0:T(1,128)S(1)}, f32[2,1,512]{2,1,0:T(1,128)S(1)}, u32[]{:S(2)}, u32[]{:S(2)}) collective-permute-start(f32[2,1,512]{2,1,0:T(1,128)S(1)} %get-tuple-element.17), channel_id=1, source_target_pairs={{1,0},{3,2},{5,4},{7,6},{9,8},{11,10},{13,12},{15,14},{17,16},{19,... | collective-permute-start | bytes 12296 | tf_op jit(solution)/shard_map/ppermute | solution.py:22
  69.4 3.8 %collective-permute-start.5 = (f32[2,1,512]{2,1,0:T(1,128)S(1)}, f32[2,1,512]{2,1,0:T(1,128)S(1)}, u32[]{:S(2)}, u32[]{:S(2)}) collective-permute-start(f32[2,1,512]{2,1,0:T(1,128)S(1)} %get-tuple-element.18), channel_id=1, source_target_pairs={{0,1},{2,3},{4,5},{6,7},{8,9},{10,11},{12,13},{14,15},{16,17},{18,... | collective-permute-start | bytes 12296 | tf_op jit(solution)/shard_map/ppermute | solution.py:21
  86.0 11.0 %all-to-all-start.2 = ((f32[16,1,1024]{2,1,0:T(1,128)}), f32[16,1,1024]{2,1,0:T(1,128)S(1)}, u32[]{:S(2)}, u32[]{:S(2)}) async-start(f32[16,1,1024]{2,1,0:T(1,128)} %reshape.140), calls=%async_computation.2 | async-start | bytes 131072 | tf_op jit(solution)/shard_map/all_to_all | solution.py:90
  105.6 24.0 %copy-start = (f32[4,2,1,8,512]{4,3,2,1,0:T(8,128)S(1)}, f32[4,2,1,8,512]{4,3,2,1,0:T(8,128)}, u32[]{:S(2)}) copy-start(f32[4,2,1,8,512]{4,3,2,1,0:T(8,128)} %param.3) | copy-start | bytes 393220
  119.8 7.8 %collective-permute-start.6 = (f32[2,8,512]{2,1,0:T(8,128)S(1)}, f32[2,8,512]{2,1,0:T(8,128)S(1)}, u32[]{:S(2)}, u32[]{:S(2)}) collective-permute-start(f32[2,8,512]{2,1,0:T(8,128)S(1)} %reshape_squeeze.15), channel_id=1, source_target_pairs={{0,2},{2,4},{4,6},{6,8},{8,10},{10,12},{12,14},{14,16},{16,18},{18... | collective-permute-start | bytes 98312 | tf_op jit(solution)/shard_map/ppermute | solution.py:30
  122.4 4.4 %collective-permute-start.7 = (f32[1,1,512]{2,1,0:T(1,128)S(1)}, f32[1,1,512]{2,1,0:T(1,128)S(1)}, u32[]{:S(2)}, u32[]{:S(2)}) collective-permute-start(f32[1,1,512]{2,1,0:T(1,128)S(1)} %get-tuple-element.29), channel_id=1, source_target_pairs={{1,0},{3,2},{5,4},{7,6},{9,8},{11,10},{13,12},{15,14},{17,16},{19,... | collective-permute-start | bytes 6152 | tf_op jit(solution)/shard_map/ppermute | solution.py:22
  123.7 3.8 %collective-permute-start.8 = (f32[1,1,512]{2,1,0:T(1,128)S(1)}, f32[1,1,512]{2,1,0:T(1,128)S(1)}, u32[]{:S(2)}, u32[]{:S(2)}) collective-permute-start(f32[1,1,512]{2,1,0:T(1,128)S(1)} %get-tuple-element.30), channel_id=1, source_target_pairs={{0,1},{2,3},{4,5},{6,7},{8,9},{10,11},{12,13},{14,15},{16,17},{18,... | collective-permute-start | bytes 6152 | tf_op jit(solution)/shard_map/ppermute | solution.py:21
where the time goes:
time: 170 us; the launch traced here: 169 us
  blocking collectives  64.5 us (38%)
  local copies, waits for them, and re-layouts  33.7 us (20%)
  starting transfers between devices  27 us (16%)
  other arithmetic  23.6 us (14%)
  waiting for transfers between devices  17.7 us (10%)
  between operations  2.06 us (1%)
    psum x1, blocking collectives, on_device(): gram = lax.psum(local_terms, ('tm', 'rows'))  39 us
    unnamed x10, local copies, waits for them, and re-layouts  22.8 us
    unnamed x1, other arithmetic  19.4 us
    all_to_all x1, blocking collectives, on_device(): lax.all_to_all(scaled.reshape(1, 2, cells), 'tm', split_axis=2, concat_ax...  15.5 us
    ppermute x4, starting transfers between devices, padded_2(): before = lax.ppermute(last, axis, up)  12.3 us
    all_to_all x1, blocking collectives, on_device(): lax.all_to_all(history, 'tm', split_axis=0, concat_axis=2, tiled=True)  9.98 us
    all_to_all x1, waiting for transfers between devices, on_device(): lax.all_to_all(yhat.reshape(1, 2, 2, cells), 'tm', split_axis=3, concat_a...  7.49 us
    all_to_all x1, waiting for transfers between devices, on_device(): lax.all_to_all(stacked, 'tm', split_axis=0, concat_axis=3, tiled=True)  7.25 us
  transfers between devices with their start and end apart: 11, of which 6 were waited for; matrix products, arithmetic and copies ran while one was open for 0% of the time, Pallas kernels for 0%

commit v1 on v0

v1 whole, which is shorter than its diff:
```python
import functools

import jax
import jax.numpy as jnp
import numpy as np
from jax import lax
from jax.experimental import pallas as pl
from jax.experimental.pallas import tpu as pltpu
from jax.sharding import PartitionSpec as P

SWEEPS = 4
ALPHA = 0.01
LANES = 128
SUB = 8
GROUP = SUB // 2
FIELDS = 2
MESH = pl.DeviceIdType.MESH


def coefficients(steps):
    kappa = 16.0 / (steps * steps)
    index = np.arange(steps)
    base = ALPHA ** (1.0 / steps)
    gamma = ALPHA ** (index / steps)
    lam = 1.0 - base * np.exp(-2j * np.pi * index / steps)
    den = lam * lam + 4.0 * kappa
    wave = np.exp(2j * np.pi * (np.outer(index, index) % steps) / steps)
    scale = gamma[None, :] / gamma[:, None] / steps
    out = np.zeros((SWEEPS, FIELDS, steps, FIELDS, steps))
    for s in range(SWEEPS):
        power = kappa**s / den ** (s + 1)
        for f in range(FIELDS):
            for g in range(FIELDS):
                symbol = power * lam ** (f + 1 - g)
                if f == 1 and g == 0 and s == 0:
                    symbol = symbol - 1.0
                kernel = ((wave * symbol) @ wave.conj().T).real
                out[s, f, :, g, :] = kernel * scale
    return out.reshape(SWEEPS * FIELDS * steps, FIELDS * steps)


def split_terms(matrix):
    rest = matrix.astype(np.float32)
    pieces = []
    for _ in range(3):
        piece = rest.astype(jnp.bfloat16)
        pieces.append(piece)
        rest = rest - piece.astype(np.float32)
    one, two, three = pieces
    return np.concatenate([one, two, three, one, two, one], axis=1)


def roll(value, shift, axis):
    size = value.shape[axis]
    if isinstance(shift, int):
        shift = shift % size
        if shift == 0:
            return value
    else:
        shift = lax.rem(shift + 2 * size, size)
    return pltpu.roll(value, shift, axis)


def kernel(steps, ranks, cols, krylov, x_hbm, b_hbm, c_hbm, z_ref, im_ref, gram_ref,
           x_ref, b_ref, c_ref, pack_own, pack_halo, pack_basis, got_own, got_halo, got_basis,
           pack_out, got_out, part, parts, in_sem, send_sem, recv_sem):
    me = lax.axis_index("tm")
    row = lax.axis_index("rows")
    other = 1 - row
    width = cols // steps
    span = width + 2 * SWEEPS
    slot = LANES // 4
    kappa = 16.0 / (steps * steps)
    planes = krylov * FIELDS
    tiles = planes // 4
    lane = lax.broadcasted_iota(jnp.int32, (SUB, LANES), 1)
    sub = lax.broadcasted_iota(jnp.int32, (SUB, LANES), 0)

    barrier = pltpu.get_barrier_semaphore()

    def greet(k, carry):
        to = lax.rem(me + k, steps)
        pl.semaphore_signal(barrier, inc=1, device_id={"tm": to, "rows": row}, device_id_type=MESH)
        pl.semaphore_signal(barrier, inc=1, device_id={"tm": to, "rows": other}, device_id_type=MESH)
        return carry

    loads = [
        pltpu.make_async_copy(x_hbm, x_ref, in_sem.at[0]),
        pltpu.make_async_copy(b_hbm, b_ref, in_sem.at[1]),
        pltpu.make_async_copy(c_hbm, c_ref, in_sem.at[2]),
    ]
    for load in loads:
        load.start()
    pl.semaphore_signal(barrier, inc=1, device_id={"tm": me, "rows": other}, device_id_type=MESH)
    lax.fori_loop(1, steps, greet, 0)

    def window(read, start, count, place):
        first = max(start, 0)
        last = min(start + count, cols)
        lo = first // LANES
        hi = (last - 1) // LANES
        shift = place - start
        at = lane - place
        value = jnp.zeros((SUB, LANES), jnp.float32)
        for tile in range(lo, hi + 1):
            left = max(first, tile * LANES) - start
            right = min(last, (tile + 1) * LANES) - start
            moved = roll(read(tile), shift + tile * LANES, 1)
            value = jnp.where((at >= left) & (at < right), moved, value)
        return value

    loads[0].wait()
    lows, highs, edges = [], [], []
    for tile in range(cols // LANES):
        at = slice(tile * LANES, (tile + 1) * LANES)
        f0, f1 = x_ref[0, :, at], x_ref[1, :, at]
        low = jnp.where(sub < GROUP, f0, roll(f1, GROUP, 0))
        high = jnp.where(sub < GROUP, roll(f0, GROUP, 0), f1)
        lows.append(low)
        highs.append(high)
        edges.append(jnp.where(row == 0, high, low))
    for to in range(steps):
        start = to * width - SWEEPS
        own = window(lambda i: lows[i], start, span, span * row)
        own = own + window(lambda i: highs[i], start, span, span * (row + 1))
        pack_own[to * SUB:(to + 1) * SUB, :] = own
        pack_halo[to * SUB:(to + 1) * SUB, :] = window(lambda i: edges[i], start, span, 2 * span * row)
    loads[1].wait()
    for to in range(steps):
        for b in range(tiles):
            value = jnp.zeros((SUB, LANES), jnp.float32)
            for m in range(4):
                plane = b * 4 + m
                read = lambda i, plane=plane: b_ref[plane // FIELDS, plane % FIELDS, :, i * LANES:(i + 1) * LANES]
                value = value + window(read, to * width, width, m * slot)
            at = (to * tiles + b) * SUB
            pack_basis[at:at + SUB, :] = value

    def block(index, size):
        return pl.ds(pl.multiple_of(index * size, size), size)

    def remote(source, target, size, to, to_row, which):
        return pltpu.make_async_remote_copy(
            src_ref=source.at[block(to, size)],
            dst_ref=target.at[block(me, size)],
            send_sem=send_sem.at[which],
            recv_sem=recv_sem.at[which],
            device_id={"tm": to, "rows": to_row},
            device_id_type=MESH,
        )

    def keep(source, target, size, which):
        pltpu.make_async_copy(source.at[block(me, size)], target.at[block(me, size)], recv_sem.at[which]).start()

    def arrived(target, which):
        pltpu.make_async_copy(target, target, recv_sem.at[which]).wait()

    def left(source, count, which):
        ref = source.at[pl.ds(0, count)]
        pltpu.make_async_copy(ref, ref, send_sem.at[which]).wait()

    pl.semaphore_wait(barrier, steps * ranks - 1)

    def send_resid(k, carry):
        to = lax.rem(me + k, steps)
        remote(pack_own, got_own, SUB, to, row, 0).start()
        remote(pack_halo, got_halo, SUB, to, other, 1).start()
        return carry

    def send_basis(k, carry):
        remote(pack_basis, got_basis, SUB * tiles, lax.rem(me + k, steps), row, 2).start()
        return carry

    lax.fori_loop(1, steps, send_resid, 0)
    remote(pack_halo, got_halo, SUB, me, other, 1).start()
    keep(pack_own, got_own, SUB, 0)
    lax.fori_loop(1, steps, send_basis, 0)
    keep(pack_basis, got_basis, SUB * tiles, 2)
    loads[2].wait()

    arrived(got_own, 0)
    arrived(got_halo, 1)
    stripes = []
    for p in range(GROUP):
        pair = []
        for f in range(FIELDS):
            at = pl.ds(f * GROUP + p, steps, stride=SUB)
            pair.append(got_own[at, :] + got_halo[at, :])
        stripes.append(jnp.concatenate(pair, axis=0))
    data = jnp.concatenate(stripes, axis=1)
    one = data.astype(jnp.bfloat16)
    rest = data - one.astype(jnp.float32)
    two = rest.astype(jnp.bfloat16)
    three = (rest - two.astype(jnp.float32)).astype(jnp.bfloat16)
    stacked = jnp.concatenate([one, one, one, two, two, three], axis=0)
    depth = FIELDS * steps

    lane2 = lax.broadcasted_iota(jnp.int32, (depth, LANES), 1)
    column = lax.rem(lane2, span) + (me * width - SWEEPS)
    inside = (column >= 0) & (column < cols) & (lane2 < 3 * span)

    def term(s):
        product = jnp.dot(c_ref[s * depth:(s + 1) * depth, :], stacked, preferred_element_type=jnp.float32)
        return [product[:, p * LANES:(p + 1) * LANES] for p in range(GROUP)]

    def near(field):
        at = lane2[: field[0].shape[0]]
        out = []
        for p in range(GROUP):
            if p > 0:
                above = field[p - 1]
            else:
                above = jnp.where(at >= span, roll(field[GROUP - 1], span, 1), 0.0)
            if p < GROUP - 1:
                below = field[p + 1]
            else:
                below = jnp.where(at < 2 * span, roll(field[0], -span, 1), 0.0)
            out.append((above + below) + (roll(field[p], 1, 1) + roll(field[p], -1, 1)))
        return out

    field = term(SWEEPS - 1)
    for s in range(SWEEPS - 2, -1, -1):
        field = [a + jnp.where(inside, b, 0.0) for a, b in zip(term(s), near(field))]

    disp = [v[:steps] for v in field]
    vel = [v[steps:] for v in field]
    later = lax.broadcasted_iota(jnp.int32, (steps, LANES), 0) > 0
    before = lambda v: jnp.where(later, roll(v, 1, 0), 0.0)
    around = near(disp)
    lane1 = lane2[:steps]
    rows_out = [None] * SUB
    for p in range(GROUP):
        first = disp[p] - before(disp[p]) - vel[p]
        second = vel[p] - before(vel[p]) - kappa * (around[p] - 4.0 * disp[p])
        for h in range(2):
            value = jnp.zeros((steps, LANES), jnp.float32)
            for m, comp in enumerate((disp[p], vel[p], first, second)):
                moved = roll(comp, m * slot - SWEEPS - span * (row + h), 1)
                value = jnp.where((lane1 >= m * slot) & (lane1 < m * slot + width), moved, value)
            q = h * GROUP + p
            rows_out[q] = value
            pack_out[pl.ds(q, steps, stride=SUB), :] = value

    def send_out(k, carry):
        remote(pack_out, got_out, SUB, lax.rem(me + k, steps), row, 3).start()
        return carry

    lax.fori_loop(1, steps, send_out, 0)
    keep(pack_out, got_out, SUB, 3)

    arrived(got_basis, 2)
    sums = [jnp.zeros((steps, LANES), jnp.float32) for _ in range(tiles + 1)]
    for q in range(SUB):
        value = rows_out[q]
        twice = jnp.where(lane1 < 2 * slot, roll(value, 2 * slot, 1), value)
        for b in range(tiles):
            sums[b] = sums[b] + twice * got_basis[pl.ds(b * SUB + q, steps, stride=SUB * tiles), :]
        sums[tiles] = sums[tiles] + twice * twice
    lane0 = lax.broadcasted_iota(jnp.int32, (1, LANES), 1)
    line = jnp.zeros((1, LANES), jnp.float32)
    total = 2.0 * steps * ranks * SUB * cols
    for b in range(tiles + 1):
        folded = jnp.sum(sums[b], axis=0, keepdims=True)
        if b < tiles:
            low = jnp.sum(jnp.where(lane0 < 2 * slot, folded, 0.0), axis=1, keepdims=True)
            high = jnp.sum(jnp.where(lane0 >= 2 * slot, folded, 0.0), axis=1, keepdims=True)
            line = jnp.where(lane0 == 2 * b, low, jnp.where(lane0 == 2 * b + 1, high, line))
        else:
            low = jnp.sum(jnp.where(lane0 < 2 * slot, folded, 0.0), axis=1, keepdims=True)
            line = jnp.where(lane0 == krylov, low * (1.0 / total), line)
    part[...] = line[None]
    mine = me * ranks + row

    def tell(to, to_row):
        pltpu.make_async_remote_copy(
            src_ref=part,
            dst_ref=parts.at[pl.ds(mine, 1)],
            send_sem=send_sem.at[4],
            recv_sem=recv_sem.at[4],
            device_id={"tm": to, "rows": to_row},
            device_id_type=MESH,
        ).start()

    def send_part(k, carry):
        to = lax.rem(me + k, steps)
        tell(to, row)
        tell(to, other)
        return carry

    lax.fori_loop(1, steps, send_part, 0)
    tell(me, other)
    pltpu.make_async_copy(part, parts.at[pl.ds(mine, 1)], recv_sem.at[4]).start()

    arrived(got_out, 3)
    per = LANES // width
    for tile in range(cols // LANES):
        values = [jnp.zeros((SUB, LANES), jnp.float32) for _ in range(4)]
        for i in range(per):
            source = tile * per + i
            got = got_out[source * SUB:(source + 1) * SUB, :]
            spot = (lane >= i * width) & (lane < (i + 1) * width)
            for m in range(4):
                values[m] = jnp.where(spot, roll(got, i * width - m * slot, 1), values[m])
        at = slice(tile * LANES, (tile + 1) * LANES)
        z_ref[0, :, at] = values[0]
        z_ref[1, :, at] = values[1]
        im_ref[0, :, at] = values[2]
        im_ref[1, :, at] = values[3]

    arrived(parts, 4)
    gram_ref[...] = jnp.sum(parts[...], axis=0)
    left(pack_own, (steps - 1) * SUB, 0)
    left(pack_halo, steps * SUB, 1)
    left(pack_basis, (steps - 1) * SUB * tiles, 2)
    left(pack_out, (steps - 1) * SUB, 3)
    left(parts, steps * ranks - 1, 4)


def solution(mesh):
    steps, ranks = mesh.shape["tm"], mesh.shape["rows"]
    table = split_terms(coefficients(steps))

    def on_device(resid, basis):
        rows_dev, cols = resid.shape[2:]
        krylov = basis.shape[0]
        width = cols // steps
        assert ranks == 2 and rows_dev == SUB and cols % LANES == 0 and cols % steps == 0
        assert LANES % width == 0 and 4 * width <= LANES and 3 * (width + 2 * SWEEPS) <= LANES
        assert (krylov * FIELDS) % 4 == 0 and steps % SUB == 0
        tiles = krylov * FIELDS // 4
        const = jnp.asarray(table)
        vmem = lambda *shape: pltpu.VMEM(shape, jnp.float32)
        plane = jax.ShapeDtypeStruct((FIELDS, rows_dev, cols), jnp.float32)
        z, image, gram = pl.pallas_call(
            functools.partial(kernel, steps, ranks, cols, krylov),
            out_shape=[plane, plane, jax.ShapeDtypeStruct((1, LANES), jnp.float32)],
            in_specs=[pl.BlockSpec(memory_space=pl.ANY)] * 3,
            out_specs=[pl.BlockSpec(memory_space=pltpu.VMEM)] * 3,
            scratch_shapes=[
                vmem(FIELDS, rows_dev, cols),
                vmem(krylov, FIELDS, rows_dev, cols),
                pltpu.VMEM(table.shape, jnp.bfloat16),
                vmem(steps * SUB, LANES),
                vmem(steps * SUB, LANES),
                vmem(steps * SUB * tiles, LANES),
                vmem(steps * SUB, LANES),
                vmem(steps * SUB, LANES),
                vmem(steps * SUB * tiles, LANES),
                vmem(steps * SUB, LANES),
                vmem(steps * SUB, LANES),
                vmem(1, 1, LANES),
                vmem(steps * ranks, 1, LANES),
                pltpu.SemaphoreType.DMA((3,)),
                pltpu.SemaphoreType.DMA((5,)),
                pltpu.SemaphoreType.DMA((5,)),
            ],
            compiler_params=pltpu.CompilerParams(collective_id=0, has_side_effects=True),
        )(resid[:, 0], basis[:, :, 0], const)
        return z[:, None], image[:, None], gram[0, : krylov + 1]

    return jax.shard_map(
        on_device,
        mesh=mesh,
        in_specs=(P(None, "tm", "rows", None), P(None, None, "tm", "rows", None)),
        out_specs=(P(None, "tm", "rows", None), P(None, "tm", "rows", None), P()),
        check_vma=False,
    )
```

time: 170 us -> 25.8 us (0.15)
  blocking collectives: 64.5 us -> 0 us
  local copies, waits for them, and re-layouts: 33.7 us -> 3.18 us
  starting transfers between devices: 27 us -> 0 us
  other arithmetic: 23.6 us -> 0 us
  Pallas kernels: 0 us -> 21.8 us
  waiting for transfers between devices: 17.7 us -> 0 us
    psum x1 -> x0, blocking collectives: 39 us -> none  [on_device(): gram = lax.psum(local_terms, ('tm', 'rows'))]
    all_to_all x2 -> x0, blocking collectives: 25.5 us -> none  [the longest x1 15.5 us: on_device(): lax.all_to_all(scaled.reshape(1, 2, cells), 'tm', split_axis=2, concat_ax...]
    pallas_call x0 -> x1, Pallas kernels: none -> 21.8 us  [on_device(): pl.pallas_call(functools.partial(kernel, steps, ranks, cols, krylov), out...]
    unnamed x10 -> x6, local copies, waits for them, and re-layouts: 22.8 us -> 2.67 us
    ppermute x9 -> x0, starting transfers between devices: 20.1 us -> none  [the longest x4 12.3 us: padded_2(): before = lax.ppermute(last, axis, up)]
    unnamed x1 -> x0, other arithmetic: 19.4 us -> none
    all_to_all x2 -> x0, waiting for transfers between devices: 14.7 us -> none  [the longest x1 7.49 us: on_device(): lax.all_to_all(yhat.reshape(1, 2, 2, cells), 'tm', split_axis=3, concat_a...]
    all_to_all x2 -> x0, starting transfers between devices: 6.98 us -> none  [the longest x1 3.49 us: on_device(): lax.all_to_all(yhat.reshape(1, 2, 2, cells), 'tm', split_axis=3, concat_a...]
  transfers between devices with their start and end apart: 11 -> 0, of which waited for: 6 -> 0; matrix products, arithmetic and copies ran while one was open for 0% -> 0% of each run, Pallas kernels for 0% -> 0%
where the time goes in v1:
time: 25.8 us; the launch traced here: 25.6 us
  Pallas kernels  21.8 us (84%)
  local copies, waits for them, and re-layouts  3.18 us (12%)
  between operations  0.65 us (3%)
    pallas_call x1, Pallas kernels, on_device(): pl.pallas_call(functools.partial(kernel, steps, ranks, cols, krylov), out...  21.8 us
    unnamed x6, local copies, waits for them, and re-layouts  2.67 us

profile of v1, /device:TPU:0, one launch (start us, length us, event | category | flops | bytes accessed | tf_op | source)
XLA Modules:
  0.0 25.6 jit_solution(2127927824018765615)
XLA Ops:
  0.6 21.8 %shard_map.58 = (f32[2,8,512]{2,1,0:T(8,128)}, f32[2,8,512]{2,1,0:T(8,128)}, f32[1,128]{1,0:T(1,128)}) custom-call(f32[2,8,512]{2,1,0:T(8,128)} %bitcast.11, f32[4,2,8,512]{3,2,1,0:T(8,128)} %bitcast.10, bf16[128,192]{1,0:T(8,128)(2,1)} %constant.2.clone.c_hbm), custom_call_target="tpu_custom_call" | custom-call | tf_op jit(solution)/shard_map/pallas_call | solution.py:334
  22.4 0.0 copy-start.1
  22.4 0.7 %copy-done.1 = f32[1,128]{1,0:T(1,128)S(1)} copy-done((f32[1,128]{1,0:T(1,128)S(1)}, f32[1,128]{1,0:T(1,128)}, u32[]{:S(2)}) %copy-start.1) | copy-done | bytes 536
  23.1 0.5 %slice_bitcast_fusion = f32[5]{0:T(128)} fusion(f32[1,128]{1,0:T(1,128)S(1)} %copy-done.1), kind=kLoop, calls=%fused_computation | loop fusion | bytes 40 | tf_op jit(solution)/shard_map/squeeze | solution.py:359
  23.6 0.0 copy-start
  23.6 1.4 %copy.10 = f32[2,1,8,512]{3,2,1,0:T(8,128)} copy(f32[2,1,8,512]{3,2,1,0:T(8,128)} %bitcast.13) | data formatting | bytes 65536
  25.0 0.0 copy-done
  25.0 0.6 %copy.11 = f32[2,1,8,512]{3,2,1,0:T(8,128)} copy(f32[2,1,8,512]{3,2,1,0:T(8,128)S(1)} %bitcast.12) | data formatting | bytes 65536
Async XLA Ops:
  22.4 0.7 %copy-start.1 = (f32[1,128]{1,0:T(1,128)S(1)}, f32[1,128]{1,0:T(1,128)}, u32[]{:S(2)}) copy-start(f32[1,128]{1,0:T(1,128)} %get-tuple-element.8) | copy-start | bytes 1540
  23.6 1.4 %copy-start = (f32[2,8,512]{2,1,0:T(8,128)S(1)}, f32[2,8,512]{2,1,0:T(8,128)}, u32[]{:S(2)}) copy-start(f32[2,8,512]{2,1,0:T(8,128)} %get-tuple-element.7) | copy-start | bytes 98308

commit v2 on v1

--- a/solution.py
+++ b/solution.py
@@ -61,9 +61,31 @@
     return pltpu.roll(value, shift, axis)
 
 
-def kernel(steps, ranks, cols, krylov, x_hbm, b_hbm, c_hbm, z_ref, im_ref, gram_ref,
+def unpack(steps, krylov, got_out, parts, z_ref, im_ref, gram_ref):
+    cols = z_ref.shape[2]
+    width = cols // steps
+    slot = LANES // 4
+    per = LANES // width
+    lane = lax.broadcasted_iota(jnp.int32, (SUB, LANES), 1)
+    for tile in range(cols // LANES):
+        values = [jnp.zeros((SUB, LANES), jnp.float32) for _ in range(4)]
+        for i in range(per):
+            source = tile * per + i
+            got = got_out[source * SUB:(source + 1) * SUB, :]
+            spot = (lane >= i * width) & (lane < (i + 1) * width)
+            for m in range(4):
+                values[m] = jnp.where(spot, roll(got, i * width - m * slot, 1), values[m])
+        at = slice(tile * LANES, (tile + 1) * LANES)
+        z_ref[0, :, at] = values[0]
+        z_ref[1, :, at] = values[1]
+        im_ref[0, :, at] = values[2]
+        im_ref[1, :, at] = values[3]
+    gram_ref[...] = jnp.sum(parts[...], axis=(0, 1))[: krylov + 1]
+
+
+def kernel(steps, ranks, cols, krylov, x_hbm, b_hbm, c_hbm, got_out, parts,
            x_ref, b_ref, c_ref, pack_own, pack_halo, pack_basis, got_own, got_halo, got_basis,
-           pack_out, got_out, part, parts, in_sem, send_sem, recv_sem):
+           pack_out, part, in_sem, send_sem, recv_sem):
     me = lax.axis_index("tm")
     row = lax.axis_index("rows")
     other = 1 - row
@@ -125,6 +147,45 @@
         own = own + window(lambda i: highs[i], start, span, span * (row + 1))
         pack_own[to * SUB:(to + 1) * SUB, :] = own
         pack_halo[to * SUB:(to + 1) * SUB, :] = window(lambda i: edges[i], start, span, 2 * span * row)
+    def block(index, size):
+        return pl.ds(pl.multiple_of(index * size, size), size)
+
+    def remote(source, target, size, to, to_row, which):
+        return pltpu.make_async_remote_copy(
+            src_ref=source.at[block(to, size)],
+            dst_ref=target.at[block(me, size)],
+            send_sem=send_sem.at[which],
+            recv_sem=recv_sem.at[which],
+            device_id={"tm": to, "rows": to_row},
+            device_id_type=MESH,
+        )
+
+    def keep(source, target, size, which):
+        pltpu.make_async_copy(source.at[block(me, size)], target.at[block(me, size)], recv_sem.at[which]).start()
+
+    def arrived(target, which):
+        pltpu.make_async_copy(target, target, recv_sem.at[which]).wait()
+
+    def left(source, count, which):
+        ref = source.at[pl.ds(0, count)]
+        pltpu.make_async_copy(ref, ref, send_sem.at[which]).wait()
+
+    pl.semaphore_wait(barrier, steps * ranks - 1)
+
+    def send_resid(k, carry):
+        to = lax.rem(me + k, steps)
+        remote(pack_own, got_own, SUB, to, row, 0).start()
+        remote(pack_halo, got_halo, SUB, to, other, 1).start()
+        return carry
+
+    def send_basis(k, carry):
+        remote(pack_basis, got_basis, SUB * tiles, lax.rem(me + k, steps), row, 2).start()
+        return carry
+
+    lax.fori_loop(1, steps, send_resid, 0)
+    remote(pack_halo, got_halo, SUB, me, other, 1).start()
+    keep(pack_own, got_own, SUB, 0)
+
     loads[1].wait()
     for to in range(steps):
         for b in range(tiles):
@@ -135,45 +196,6 @@
                 value = value + window(read, to * width, width, m * slot)
             at = (to * tiles + b) * SUB
             pack_basis[at:at + SUB, :] = value
-
-    def block(index, size):
-        return pl.ds(pl.multiple_of(index * size, size), size)
-
-    def remote(source, target, size, to, to_row, which):
-        return pltpu.make_async_remote_copy(
-            src_ref=source.at[block(to, size)],
-            dst_ref=target.at[block(me, size)],
-            send_sem=send_sem.at[which],
-            recv_sem=recv_sem.at[which],
-            device_id={"tm": to, "rows": to_row},
-            device_id_type=MESH,
-        )
-
-    def keep(source, target, size, which):
-        pltpu.make_async_copy(source.at[block(me, size)], target.at[block(me, size)], recv_sem.at[which]).start()
-
-    def arrived(target, which):
-        pltpu.make_async_copy(target, target, recv_sem.at[which]).wait()
-
-    def left(source, count, which):
-        ref = source.at[pl.ds(0, count)]
-        pltpu.make_async_copy(ref, ref, send_sem.at[which]).wait()
-
-    pl.semaphore_wait(barrier, steps * ranks - 1)
-
-    def send_resid(k, carry):
-        to = lax.rem(me + k, steps)
-        remote(pack_own, got_own, SUB, to, row, 0).start()
-        remote(pack_halo, got_halo, SUB, to, other, 1).start()
-        return carry
-
-    def send_basis(k, carry):
-        remote(pack_basis, got_basis, SUB * tiles, lax.rem(me + k, steps), row, 2).start()
-        return carry
-
-    lax.fori_loop(1, steps, send_resid, 0)
-    remote(pack_halo, got_halo, SUB, me, other, 1).start()
-    keep(pack_own, got_own, SUB, 0)
     lax.fori_loop(1, steps, send_basis, 0)
     keep(pack_basis, got_basis, SUB * tiles, 2)
     loads[2].wait()
@@ -292,23 +314,7 @@
     pltpu.make_async_copy(part, parts.at[pl.ds(mine, 1)], recv_sem.at[4]).start()
 
     arrived(got_out, 3)
-    per = LANES // width
-    for tile in range(cols // LANES):
-        values = [jnp.zeros((SUB, LANES), jnp.float32) for _ in range(4)]
-        for i in range(per):
-            source = tile * per + i
-            got = got_out[source * SUB:(source + 1) * SUB, :]
-            spot = (lane >= i * width) & (lane < (i + 1) * width)
-            for m in range(4):
-                values[m] = jnp.where(spot, roll(got, i * width - m * slot, 1), values[m])
-        at = slice(tile * LANES, (tile + 1) * LANES)
-        z_ref[0, :, at] = values[0]
-        z_ref[1, :, at] = values[1]
-        im_ref[0, :, at] = values[2]
-        im_ref[1, :, at] = values[3]
-
     arrived(parts, 4)
-    gram_ref[...] = jnp.sum(parts[...], axis=0)
     left(pack_own, (steps - 1) * SUB, 0)
     left(pack_halo, steps * SUB, 1)
     left(pack_basis, (steps - 1) * SUB * tiles, 2)
@@ -329,13 +335,17 @@
         assert (krylov * FIELDS) % 4 == 0 and steps % SUB == 0
         tiles = krylov * FIELDS // 4
         const = jnp.asarray(table)
+        limit = 32 * 1024 * 1024
         vmem = lambda *shape: pltpu.VMEM(shape, jnp.float32)
         plane = jax.ShapeDtypeStruct((FIELDS, rows_dev, cols), jnp.float32)
-        z, image, gram = pl.pallas_call(
+        got, parts = pl.pallas_call(
             functools.partial(kernel, steps, ranks, cols, krylov),
-            out_shape=[plane, plane, jax.ShapeDtypeStruct((1, LANES), jnp.float32)],
-            in_specs=[pl.BlockSpec(memory_space=pl.ANY)] * 3,
-            out_specs=[pl.BlockSpec(memory_space=pltpu.VMEM)] * 3,
+            out_shape=[
+                jax.ShapeDtypeStruct((steps * SUB, LANES), jnp.float32),
+                jax.ShapeDtypeStruct((steps * ranks, 1, LANES), jnp.float32),
+            ],
+            in_specs=[pl.BlockSpec(memory_space=pltpu.HBM)] * 3,
+            out_specs=[pl.BlockSpec(memory_space=pl.ANY)] * 2,
             scratch_shapes=[
                 vmem(FIELDS, rows_dev, cols),
                 vmem(krylov, FIELDS, rows_dev, cols),
@@ -347,16 +357,21 @@
                 vmem(steps * SUB, LANES),
                 vmem(steps * SUB * tiles, LANES),
                 vmem(steps * SUB, LANES),
-                vmem(steps * SUB, LANES),
                 vmem(1, 1, LANES),
-                vmem(steps * ranks, 1, LANES),
                 pltpu.SemaphoreType.DMA((3,)),
                 pltpu.SemaphoreType.DMA((5,)),
                 pltpu.SemaphoreType.DMA((5,)),
             ],
-            compiler_params=pltpu.CompilerParams(collective_id=0, has_side_effects=True),
+            compiler_params=pltpu.CompilerParams(collective_id=0, has_side_effects=True, vmem_limit_bytes=limit),
         )(resid[:, 0], basis[:, :, 0], const)
-        return z[:, None], image[:, None], gram[0, : krylov + 1]
+        z, image, gram = pl.pallas_call(
+            functools.partial(unpack, steps, krylov),
+            out_shape=[plane, plane, jax.ShapeDtypeStruct((krylov + 1,), jnp.float32)],
+            in_specs=[pl.BlockSpec(memory_space=pltpu.VMEM)] * 2,
+            out_specs=[pl.BlockSpec(memory_space=pltpu.VMEM)] * 3,
+            compiler_params=pltpu.CompilerParams(vmem_limit_bytes=limit),
+        )(got, parts)
+        return z[:, None], image[:, None], gram
 
     return jax.shard_map(
         on_device,

time: 25.8 us -> 25.5 us (0.988)
  local copies, waits for them, and re-layouts: 3.18 us -> 2.49 us
  Pallas kernels: 21.8 us -> 22.1 us
    pallas_call x0 -> x1, Pallas kernels: none -> 0.74 us  [on_device(): pl.pallas_call(functools.partial(unpack, steps, krylov), out_shape=[plane...]
    squeeze x1 -> x0, local copies, waits for them, and re-layouts: 0.51 us -> none  [on_device(): return (z[:, None], image[:, None], gram[0, :krylov + 1])]
    pallas_call x1, Pallas kernels: 21.8 us -> 21.4 us  [on_device(): pl.pallas_call(functools.partial(kernel, steps, ranks, cols, krylov), out...]
where the time goes in v2:
time: 25.5 us; the launch traced here: 25.3 us
  Pallas kernels  22.1 us (87%)
  local copies, waits for them, and re-layouts  2.49 us (10%)
  between operations  0.65 us (3%)
    pallas_call x1, Pallas kernels, on_device(): pl.pallas_call(functools.partial(kernel, steps, ranks, cols, krylov), out...  21.4 us
    unnamed x6, local copies, waits for them, and re-layouts  2.49 us
    pallas_call x1, Pallas kernels, on_device(): pl.pallas_call(functools.partial(unpack, steps, krylov), out_shape=[plane...  0.74 us

profile of v2, /device:TPU:0, one launch (start us, length us, event | category | flops | bytes accessed | tf_op | source)
XLA Modules:
  0.0 25.3 jit_solution(553198215897315222)
XLA Ops:
  0.6 0.0 copy-start
  0.6 0.9 %copy-done = f32[4,2,1,8,512]{4,3,2,1,0:T(8,128)S(1)} copy-done((f32[4,2,1,8,512]{4,3,2,1,0:T(8,128)S(1)}, f32[4,2,1,8,512]{4,3,2,1,0:T(8,128)}, u32[]{:S(2)}) %copy-start) | copy-done | bytes 131096
  1.5 0.0 copy-start.1
  1.5 0.8 %copy-done.1 = bf16[128,192]{1,0:T(8,128)(2,1)S(1)} copy-done((bf16[128,192]{1,0:T(8,128)(2,1)S(1)}, bf16[128,192]{1,0:T(8,128)(2,1)}, u32[]{:S(2)}) %copy-start.1) | copy-done | bytes 49176
  2.4 0.0 copy-start.2
  2.4 0.8 %copy-done.2 = f32[2,1,8,512]{3,2,1,0:T(8,128)S(1)} copy-done((f32[2,1,8,512]{3,2,1,0:T(8,128)S(1)}, f32[2,1,8,512]{3,2,1,0:T(8,128)}, u32[]{:S(2)}) %copy-start.2) | copy-done | bytes 32792
  3.1 21.4 %shard_map.58 = (f32[128,128]{1,0:T(8,128)S(1)}, f32[32,1,128]{2,1,0:T(1,128)S(1)}) custom-call(f32[2,8,512]{2,1,0:T(8,128)S(1)} %bitcast.9, f32[4,2,8,512]{3,2,1,0:T(8,128)S(1)} %bitcast.8, bf16[128,192]{1,0:T(8,128)(2,1)S(1)} %copy-done.1), custom_call_target="tpu_custom_call" | custom-call | tf_op jit(solution)/shard_map/pallas_call | solution.py:341
  24.5 0.7 %shard_map.59 = (f32[2,8,512]{2,1,0:T(8,128)}, f32[2,8,512]{2,1,0:T(8,128)}, f32[5]{0:T(128)}) custom-call(f32[128,128]{1,0:T(8,128)S(1)} %get-tuple-element.8.got_out, f32[32,1,128]{2,1,0:T(1,128)S(1)} %get-tuple-element.9.parts), custom_call_target="tpu_custom_call" | custom-call | tf_op jit(solution)/shard_map/pallas_call | solution.py:367
Async XLA Ops:
  0.6 0.9 %copy-start = (f32[4,2,1,8,512]{4,3,2,1,0:T(8,128)S(1)}, f32[4,2,1,8,512]{4,3,2,1,0:T(8,128)}, u32[]{:S(2)}) copy-start(f32[4,2,1,8,512]{4,3,2,1,0:T(8,128)} %param.4) | copy-start | bytes 393220
  1.5 0.8 %copy-start.1 = (bf16[128,192]{1,0:T(8,128)(2,1)S(1)}, bf16[128,192]{1,0:T(8,128)(2,1)}, u32[]{:S(2)}) copy-start(bf16[128,192]{1,0:T(8,128)(2,1)} %constant.2.clone.c_hbm) | copy-start | bytes 147460
  2.4 0.8 %copy-start.2 = (f32[2,1,8,512]{3,2,1,0:T(8,128)S(1)}, f32[2,1,8,512]{3,2,1,0:T(8,128)}, u32[]{:S(2)}) copy-start(f32[2,1,8,512]{3,2,1,0:T(8,128)} %param.3) | copy-start | bytes 98308

commit v3 on v2

--- a/solution.py
+++ b/solution.py
@@ -100,8 +100,11 @@
 
     barrier = pltpu.get_barrier_semaphore()
 
+    def peer(k):
+        return lax.rem(me + lax.rem(k + steps // 2 - 2, steps - 1) + 1, steps)
+
     def greet(k, carry):
-        to = lax.rem(me + k, steps)
+        to = peer(k)
         pl.semaphore_signal(barrier, inc=1, device_id={"tm": to, "rows": row}, device_id_type=MESH)
         pl.semaphore_signal(barrier, inc=1, device_id={"tm": to, "rows": other}, device_id_type=MESH)
         return carry
@@ -173,13 +176,13 @@
     pl.semaphore_wait(barrier, steps * ranks - 1)
 
     def send_resid(k, carry):
-        to = lax.rem(me + k, steps)
+        to = peer(k)
         remote(pack_own, got_own, SUB, to, row, 0).start()
         remote(pack_halo, got_halo, SUB, to, other, 1).start()
         return carry
 
     def send_basis(k, carry):
-        remote(pack_basis, got_basis, SUB * tiles, lax.rem(me + k, steps), row, 2).start()
+        remote(pack_basis, got_basis, SUB * tiles, peer(k), row, 2).start()
         return carry
 
     lax.fori_loop(1, steps, send_resid, 0)
@@ -264,7 +267,7 @@
             pack_out[pl.ds(q, steps, stride=SUB), :] = value
 
     def send_out(k, carry):
-        remote(pack_out, got_out, SUB, lax.rem(me + k, steps), row, 3).start()
+        remote(pack_out, got_out, SUB, peer(k), row, 3).start()
         return carry
 
     lax.fori_loop(1, steps, send_out, 0)
@@ -304,7 +307,7 @@
         ).start()
 
     def send_part(k, carry):
-        to = lax.rem(me + k, steps)
+        to = peer(k)
         tell(to, row)
         tell(to, other)
         return carry
@@ -335,7 +338,7 @@
         assert (krylov * FIELDS) % 4 == 0 and steps % SUB == 0
         tiles = krylov * FIELDS // 4
         const = jnp.asarray(table)
-        limit = 32 * 1024 * 1024
+        limit = 55100 * 1024
         vmem = lambda *shape: pltpu.VMEM(shape, jnp.float32)
         plane = jax.ShapeDtypeStruct((FIELDS, rows_dev, cols), jnp.float32)
         got, parts = pl.pallas_call(
@@ -369,7 +372,7 @@
             out_shape=[plane, plane, jax.ShapeDtypeStruct((krylov + 1,), jnp.float32)],
             in_specs=[pl.BlockSpec(memory_space=pltpu.VMEM)] * 2,
             out_specs=[pl.BlockSpec(memory_space=pltpu.VMEM)] * 3,
-            compiler_params=pltpu.CompilerParams(vmem_limit_bytes=limit),
+            compiler_params=pltpu.CompilerParams(vmem_limit_bytes=32 * 1024 * 1024),
         )(got, parts)
         return z[:, None], image[:, None], gram
 

time: 25.5 us -> 22.7 us (0.89)
  local copies, waits for them, and re-layouts: 2.49 us -> 0.75 us
  Pallas kernels: 22.1 us -> 21.1 us
    unnamed x6 -> x2, local copies, waits for them, and re-layouts: 2.49 us -> 0.75 us
    pallas_call x1, Pallas kernels: 21.4 us -> 20.4 us  [on_device(): pl.pallas_call(functools.partial(kernel, steps, ranks, cols, krylov), out...]
where the time goes in v3:
time: 22.7 us; the launch traced here: 22.5 us
  Pallas kernels  21.1 us (93%)
  local copies, waits for them, and re-layouts  0.75 us (3%)
  between operations  0.65 us (3%)
    pallas_call x1, Pallas kernels, on_device(): pl.pallas_call(functools.partial(kernel, steps, ranks, cols, krylov), out...  20.4 us
    unnamed x2, local copies, waits for them, and re-layouts  0.75 us
    pallas_call x1, Pallas kernels, on_device(): pl.pallas_call(functools.partial(unpack, steps, krylov), out_shape=[plane...  0.74 us

profile of v3, /device:TPU:0, one launch (start us, length us, event | category | flops | bytes accessed | tf_op | source)
XLA Modules:
  0.0 22.5 jit_solution(18425170825546830233)
XLA Ops:
  0.6 0.0 copy-start
  0.6 0.7 %copy-done = f32[2,1,8,512]{3,2,1,0:T(8,128)S(1)} copy-done((f32[2,1,8,512]{3,2,1,0:T(8,128)S(1)}, f32[2,1,8,512]{3,2,1,0:T(8,128)}, u32[]{:S(2)}) %copy-start) | copy-done | bytes 32792
  1.4 20.4 %shard_map.58 = (f32[128,128]{1,0:T(8,128)S(1)}, f32[32,1,128]{2,1,0:T(1,128)S(1)}) custom-call(f32[2,8,512]{2,1,0:T(8,128)S(1)} %bitcast.8, f32[4,2,8,512]{3,2,1,0:T(8,128)} %bitcast.9, bf16[128,192]{1,0:T(8,128)(2,1)} %constant.2.clone.c_hbm), custom_call_target="tpu_custom_call" | custom-call | tf_op jit(solution)/shard_map/pallas_call | solution.py:344
  21.8 0.7 %shard_map.59 = (f32[2,8,512]{2,1,0:T(8,128)}, f32[2,8,512]{2,1,0:T(8,128)}, f32[5]{0:T(128)}) custom-call(f32[128,128]{1,0:T(8,128)S(1)} %get-tuple-element.8.got_out, f32[32,1,128]{2,1,0:T(1,128)S(1)} %get-tuple-element.9.parts), custom_call_target="tpu_custom_call" | custom-call | tf_op jit(solution)/shard_map/pallas_call | solution.py:370
Async XLA Ops:
  0.6 0.8 %copy-start = (f32[2,1,8,512]{3,2,1,0:T(8,128)S(1)}, f32[2,1,8,512]{3,2,1,0:T(8,128)}, u32[]{:S(2)}) copy-start(f32[2,1,8,512]{3,2,1,0:T(8,128)} %param.3) | copy-start | bytes 98308

commit v4 on v3

--- a/solution.py
+++ b/solution.py
@@ -178,7 +178,10 @@
     def send_resid(k, carry):
         to = peer(k)
         remote(pack_own, got_own, SUB, to, row, 0).start()
-        remote(pack_halo, got_halo, SUB, to, other, 1).start()
+        return carry
+
+    def send_halo(k, carry):
+        remote(pack_halo, got_halo, SUB, peer(k), other, 1).start()
         return carry
 
     def send_basis(k, carry):
@@ -186,6 +189,7 @@
         return carry
 
     lax.fori_loop(1, steps, send_resid, 0)
+    lax.fori_loop(1, steps, send_halo, 0)
     remote(pack_halo, got_halo, SUB, me, other, 1).start()
     keep(pack_own, got_own, SUB, 0)
 

time: 22.7 us -> 22.6 us (level)
  no operation moved by 1% of the time
where the time goes in v4:
time: 22.6 us; the launch traced here: 22.4 us
  Pallas kernels  21 us (93%)
  local copies, waits for them, and re-layouts  0.75 us (3%)
  between operations  0.65 us (3%)
    pallas_call x1, Pallas kernels, on_device(): pl.pallas_call(functools.partial(kernel, steps, ranks, cols, krylov), out...  20.3 us
    unnamed x2, local copies, waits for them, and re-layouts  0.75 us
    pallas_call x1, Pallas kernels, on_device(): pl.pallas_call(functools.partial(unpack, steps, krylov), out_shape=[plane...  0.74 us

profile of v4, /device:TPU:0, one launch (start us, length us, event | category | flops | bytes accessed | tf_op | source)
XLA Modules:
  0.0 22.4 jit_solution(16301155699379921123)
XLA Ops:
  0.6 0.0 copy-start
  0.6 0.7 %copy-done = f32[2,1,8,512]{3,2,1,0:T(8,128)S(1)} copy-done((f32[2,1,8,512]{3,2,1,0:T(8,128)S(1)}, f32[2,1,8,512]{3,2,1,0:T(8,128)}, u32[]{:S(2)}) %copy-start) | copy-done | bytes 32792
  1.4 20.3 %shard_map.58 = (f32[128,128]{1,0:T(8,128)S(1)}, f32[32,1,128]{2,1,0:T(1,128)S(1)}) custom-call(f32[2,8,512]{2,1,0:T(8,128)S(1)} %bitcast.8, f32[4,2,8,512]{3,2,1,0:T(8,128)} %bitcast.9, bf16[128,192]{1,0:T(8,128)(2,1)} %constant.2.clone.c_hbm), custom_call_target="tpu_custom_call" | custom-call | tf_op jit(solution)/shard_map/pallas_call | solution.py:348
  21.6 0.7 %shard_map.59 = (f32[2,8,512]{2,1,0:T(8,128)}, f32[2,8,512]{2,1,0:T(8,128)}, f32[5]{0:T(128)}) custom-call(f32[128,128]{1,0:T(8,128)S(1)} %get-tuple-element.8.got_out, f32[32,1,128]{2,1,0:T(1,128)S(1)} %get-tuple-element.9.parts), custom_call_target="tpu_custom_call" | custom-call | tf_op jit(solution)/shard_map/pallas_call | solution.py:374
Async XLA Ops:
  0.6 0.8 %copy-start = (f32[2,1,8,512]{3,2,1,0:T(8,128)S(1)}, f32[2,1,8,512]{3,2,1,0:T(8,128)}, u32[]{:S(2)}) copy-start(f32[2,1,8,512]{3,2,1,0:T(8,128)} %param.3) | copy-start | bytes 98308
